TPU v7x, 32 devices: a whole 2x2x4 slice. The times are simulated.
32 devices in a mesh: section: 4 (over y, x), fsdp: 8 (over z, core).
Axes of the slice: x: 2, y: 2, z: 4, core: 2. Of those that a mesh axis runs over, the one named last changes fastest.
Arguments:
- master: float32 [4, 64, 4096], P('section', 'fsdp'), may hold values from -0.12 to 0.12
- first_moment: float32 [4, 64, 4096], P('section', 'fsdp'), may hold values from -0.2 to 0.2
- second_moment: float32 [4, 64, 4096], P('section', 'fsdp'), may hold values from 0.25 to 1
- gradient: float32 [4, 64, 4096], P('section', 'fsdp'), may hold values from -64 to 64
Outputs:
- new_master: float32 [4, 64, 4096], P('section', 'fsdp')
- new_first: float32 [4, 64, 4096], P('section', 'fsdp')
- new_second: float32 [4, 64, 4096], P('section', 'fsdp')
- weights: bfloat16 [4, 64, 4096], P('section')
- grad_rms: float32 [], replicated
All inputs are finite; a program needn't handle non-finite values.
Results may differ from a plain program's by a relative error of at most 0.001.
Values may be sent and summed in bfloat16 or wider, within the bound.
A program may use at most 64 MiB of HBM per device.

v0:
```python
import jax
import jax.numpy as jnp
from jax import lax
from jax.sharding import PartitionSpec as P

BETA_ONE = 0.9
BETA_TWO = 0.95
LEARN_RATE = 0.05
DECAY = 0.1
EPSILON = 1e-08
BIAS_STEPS = 10.0


def adamw_part(master, first_moment, second_moment, gradient, clip_scale):
    scaled = clip_scale * gradient
    new_first = BETA_ONE * first_moment + (1.0 - BETA_ONE) * scaled
    new_second = BETA_TWO * second_moment + (1.0 - BETA_TWO) * scaled * scaled
    first_hat = new_first / (1.0 - BETA_ONE**BIAS_STEPS)
    second_hat = new_second / (1.0 - BETA_TWO**BIAS_STEPS)
    update = first_hat / (jnp.sqrt(second_hat) + EPSILON)
    new_master = master * (1.0 - LEARN_RATE * DECAY) - LEARN_RATE * update
    return (new_master, new_first, new_second)


def local(master, first_moment, second_moment, gradient):
    partial_sq = jnp.sum(gradient * gradient)
    within = lax.psum(partial_sq, "fsdp")
    squares = lax.psum(within, "section")
    grad_norm = jnp.sqrt(squares)
    param_count = float(
        lax.axis_size("section")
        * lax.axis_size("fsdp")
        * gradient.shape[0]
        * gradient.shape[1]
        * gradient.shape[2]
    )
    limit = jnp.float32(0.5 * param_count**0.5)
    clip_scale = limit / jnp.maximum(grad_norm, limit)
    grad_rms = grad_norm / jnp.float32(param_count**0.5)
    new_master, new_first, new_second = adamw_part(
        master, first_moment, second_moment, gradient, clip_scale
    )
    weights = lax.all_gather(new_master.astype(jnp.bfloat16), "fsdp", axis=1, tiled=True)
    return (new_master, new_first, new_second, weights, grad_rms)


def solution(mesh):
    placed = (
        P("section", "fsdp", None),
        P("section", "fsdp", None),
        P("section", "fsdp", None),
        P("section", "fsdp", None),
    )
    return jax.shard_map(
        local,
        mesh=mesh,
        in_specs=placed,
        out_specs=(
            P("section", "fsdp", None),
            P("section", "fsdp", None),
            P("section", "fsdp", None),
            P("section", None, None),
            P(),
        ),
        check_vma=False,
    )
```

profile of v0, /device:TPU:0, one launch (start us, length us, event | category | flops | bytes accessed | tf_op | source)
XLA Modules:
  0.0 50.9 jit_solution(5301626764726928907)
XLA Ops:
  0.6 0.0 copy-start
  0.6 1.6 %multiply_reduce_fusion = f32[]{:T(128)} fusion(f32[1,8,4096]{2,1,0:T(8,128)} %param.7), kind=kLoop, calls=%fused_computation.4 | loop fusion | flops 65535 | bytes 131076 | tf_op jit(solution)/shard_map/reduce_sum | solution.py:26
  2.2 18.7 %psum.14 = f32[]{:T(128)} all-reduce(f32[]{:T(128)} %multiply_reduce_fusion), channel_id=1, replica_groups=mesh['section'=4,'fsdp'=8] {'fsdp'}, use_global_device_ids=true, to_apply=%region_1.0 | all-reduce | flops 1 | bytes 8 | tf_op jit(solution)/shard_map/psum | solution.py:27
  21.0 10.5 %psum.15 = f32[]{:T(128)} all-reduce(f32[]{:T(128)} %psum.14), channel_id=1, replica_groups=mesh['section'=4,'fsdp'=8] {'section'}, use_global_device_ids=true, to_apply=%region_2.0 | all-reduce | flops 1 | bytes 8 | tf_op jit(solution)/shard_map/psum | solution.py:28
  32.2 0.0 copy-done
  32.2 1.8 %fusion.1 = (bf16[1,8,4096]{2,1,0:T(8,128)(2,1)S(1)}, f32[1,8,4096]{2,1,0:T(8,128)}, f32[1,8,4096]{2,1,0:T(8,128)}, f32[1,8,4096]{2,1,0:T(8,128)}) fusion(f32[1,8,4096]{2,1,0:T(8,128)} %param.4, f32[1,8,4096]{2,1,0:T(8,128)S(1)} %copy-done, f32[]{:T(128)S(6)} %div.21, f32[1,8,4096]{2,1,0:T(8,128)} %param.5, f32[1,8,4096]{2,1,0:T(8,128)} %param.6), kind=kLoop, calls=%fused_computation.5 | loop fusion | flops 524288 | bytes 983044 | tf_op jit(solution)/shard_map/convert_element_type | solution.py:43
  34.1 14.9 %all_gather.3 = bf16[1,64,4096]{2,1,0:T(8,128)(2,1)S(1)} all-gather(bf16[1,8,4096]{2,1,0:T(8,128)(2,1)S(1)} %get-tuple-element.5), channel_id=1, replica_groups=mesh['section'=4,'fsdp'=8] {'fsdp'}, dimensions={1}, use_global_device_ids=true | all-gather | bytes 589824 | tf_op jit(solution)/shard_map/all_gather | solution.py:43
  49.0 0.8 %copy.10 = bf16[1,64,4096]{2,1,0:T(8,128)(2,1)} copy(bf16[1,64,4096]{2,1,0:T(8,128)(2,1)S(1)} %all_gather.3) | data formatting | bytes 1048576
Async XLA Ops:
  0.6 31.6 %copy-start = (f32[1,8,4096]{2,1,0:T(8,128)S(1)}, f32[1,8,4096]{2,1,0:T(8,128)}, u32[]{:S(2)}) copy-start(f32[1,8,4096]{2,1,0:T(8,128)} %param.7) | copy-start | bytes 393220
where the time goes:
time: 51.1 us; the launch traced here: 50.9 us
  blocking collectives  44.2 us (86%)
  other arithmetic  3.44 us (7%)
  between operations  2.51 us (5%)
  local copies, waits for them, and re-layouts  0.8 us (2%)
    psum x1, blocking collectives, local(): within = lax.psum(partial_sq, 'fsdp')  18.7 us
    all_gather x1, blocking collectives, local(): lax.all_gather(new_master.astype(jnp.bfloat16), 'fsdp', axis=1, tiled=True)  14.9 us
    psum x1, blocking collectives, local(): squares = lax.psum(within, 'section')  10.5 us
    convert_element_type x1, other arithmetic, local(): new_master.astype(jnp.bfloat16)  1.83 us
    reduce_sum x1, other arithmetic, local(): partial_sq = jnp.sum(gradient * gradient)  1.61 us

commit v1 on v0

--- a/solution.py
+++ b/solution.py
@@ -25,7 +25,7 @@
 def local(master, first_moment, second_moment, gradient):
     partial_sq = jnp.sum(gradient * gradient)
     within = lax.psum(partial_sq, "fsdp")
-    squares = lax.psum(within, "section")
+    squares = jnp.sum(lax.all_gather(within, "section"), axis=0)
     grad_norm = jnp.sqrt(squares)
     param_count = float(
         lax.axis_size("section")

time: 51.1 us -> 53.1 us (1.039)
  local copies, waits for them, and re-layouts: 0.8 us -> 2.79 us
  blocking collectives: 44.2 us -> 43.5 us
  other arithmetic: 3.44 us -> 4.04 us
    psum x1 -> x0, blocking collectives: 10.5 us -> none  [local(): squares = lax.psum(within, 'section')]
    unnamed x0 -> x1, blocking collectives: none -> 9.88 us
    unnamed x3 -> x8, local copies, waits for them, and re-layouts: 0.8 us -> 2.79 us
    reduce_sum x0 -> x1, other arithmetic: none -> 0.6 us  [local(): squares = jnp.sum(lax.all_gather(within, 'section'), axis=0)]
where the time goes in v1:
time: 53.1 us; the launch traced here: 52.9 us
  blocking collectives  43.5 us (82%)
  other arithmetic  4.04 us (8%)
  local copies, waits for them, and re-layouts  2.79 us (5%)
  between operations  2.52 us (5%)
    psum x1, blocking collectives, local(): within = lax.psum(partial_sq, 'fsdp')  18.7 us
    all_gather x1, blocking collectives, local(): lax.all_gather(new_master.astype(jnp.bfloat16), 'fsdp', axis=1, tiled=True)  14.9 us
    unnamed x1, blocking collectives  9.88 us
    unnamed x8, local copies, waits for them, and re-layouts  2.79 us
    convert_element_type x1, other arithmetic, local(): new_master.astype(jnp.bfloat16)  1.83 us
    reduce_sum x1, other arithmetic, local(): partial_sq = jnp.sum(gradient * gradient)  1.6 us

profile of v1, /device:TPU:0, one launch (start us, length us, event | category | flops | bytes accessed | tf_op | source)
XLA Modules:
  0.0 52.9 jit_solution(12788073690955085228)
XLA Ops:
  0.6 0.0 copy-start
  0.6 1.6 %multiply_reduce_fusion = f32[]{:T(128)} fusion(f32[1,8,4096]{2,1,0:T(8,128)} %param.7), kind=kLoop, calls=%fused_computation.4 | loop fusion | flops 65535 | bytes 131076 | tf_op jit(solution)/shard_map/reduce_sum | solution.py:26
  2.2 0.0 copy-start.1
  2.2 18.7 %psum.7 = f32[1]{0:T(128)} all-reduce(f32[1]{0:T(128)} %bitcast), channel_id=1, replica_groups=mesh['section'=4,'fsdp'=8] {'fsdp'}, use_global_device_ids=true, to_apply=%region_1.0 | all-reduce | flops 1 | bytes 8 | tf_op jit(solution)/shard_map/psum | solution.py:27
  21.0 0.0 copy-done.1
  21.0 0.6 %dynamic-slice = u32[1]{0:T(128)} dynamic-slice(u32[32]{0:T(128)S(1)} %copy-done.1, u32[]{:T(128)S(6)} %add.18), dynamic_slice_sizes={1} | dynamic-slice | bytes 12
  21.6 1.4 %dynamic-update-slice = f32[4]{0:T(128)S(1)} dynamic-update-slice(f32[4]{0:T(128)S(1)} %broadcast.6, f32[1]{0:T(128)} %psum.7, u32[]{:T(128)} %bitcast.1) | dynamic-update-slice | bytes 12
  23.0 9.9 %all-reduce = f32[4]{0:T(128)S(1)} all-reduce(f32[4]{0:T(128)S(1)} %dynamic-update-slice), channel_id=1, replica_groups=mesh['section'=4,'fsdp'=8] {'section'}, use_global_device_ids=true, to_apply=%add | all-reduce | flops 4 | bytes 32
  32.8 0.6 %reduce_sum.19 = f32[]{:T(128)} reduce(f32[4]{0:T(128)S(1)} %all-reduce, f32[]{:T(128)} %constant.6.clone.1), dimensions={0}, to_apply=%region_2.0 | reduce | flops 3 | bytes 24 | tf_op jit(solution)/shard_map/reduce_sum | solution.py:28
  34.2 0.0 copy-done
  34.2 1.8 %fusion.1 = (bf16[1,8,4096]{2,1,0:T(8,128)(2,1)S(1)}, f32[1,8,4096]{2,1,0:T(8,128)}, f32[1,8,4096]{2,1,0:T(8,128)}, f32[1,8,4096]{2,1,0:T(8,128)}) fusion(f32[1,8,4096]{2,1,0:T(8,128)} %param.4, f32[1,8,4096]{2,1,0:T(8,128)S(1)} %copy-done, f32[]{:T(128)S(6)} %div.21, f32[1,8,4096]{2,1,0:T(8,128)} %param.5, f32[1,8,4096]{2,1,0:T(8,128)} %param.6), kind=kLoop, calls=%fused_computation.5 | loop fusion | flops 524288 | bytes 983044 | tf_op jit(solution)/shard_map/convert_element_type | solution.py:43
  36.0 14.9 %all_gather.11 = bf16[1,64,4096]{2,1,0:T(8,128)(2,1)S(1)} all-gather(bf16[1,8,4096]{2,1,0:T(8,128)(2,1)S(1)} %get-tuple-element.5), channel_id=1, replica_groups=mesh['section'=4,'fsdp'=8] {'fsdp'}, dimensions={1}, use_global_device_ids=true | all-gather | bytes 589824 | tf_op jit(solution)/shard_map/all_gather | solution.py:43
  50.9 0.8 %copy.11 = bf16[1,64,4096]{2,1,0:T(8,128)(2,1)} copy(bf16[1,64,4096]{2,1,0:T(8,128)(2,1)S(1)} %all_gather.11) | data formatting | bytes 1048576
  (1 shorter events, 0.0 us)
Async XLA Ops:
  0.6 33.5 %copy-start = (f32[1,8,4096]{2,1,0:T(8,128)S(1)}, f32[1,8,4096]{2,1,0:T(8,128)}, u32[]{:S(2)}) copy-start(f32[1,8,4096]{2,1,0:T(8,128)} %param.7) | copy-start | bytes 393220
  2.2 18.7 %copy-start.1 = (u32[32]{0:T(128)S(1)}, u32[32]{0:T(128)}, u32[]{:S(2)}) copy-start(u32[32]{0:T(128)} %constant.31) | copy-start | bytes 388
